TPU v7x, 128 devices: a whole 4x4x4 slice. The times are simulated.
128 devices in a mesh: dp: 16 (over z, y), ep: 8 (over x, core).
Axes of the slice: x: 4, y: 4, z: 4, core: 2. Of those that a mesh axis runs over, the one named last changes fastest.
Arguments:
- hidden: bfloat16 [8192, 2304], P(('dp', 'ep'))
- grad_out: bfloat16 [8192, 2304], P(('dp', 'ep'))
- expert_ids: int32 [8192, 2], P(('dp', 'ep'))
- norm_gain: float32 [2304], replicated
- w_router: float32 [2304, 8], replicated
- w_gate: bfloat16 [8, 2304, 5760], P('ep')
- w_up: bfloat16 [8, 2304, 5760], P('ep')
- w_down: bfloat16 [8, 5760, 2304], P('ep')
Outputs:
- output 1: bfloat16 [8192, 2304], P(('dp', 'ep'))
- output 2: float32 [], replicated
- output 3: bfloat16 [8192, 2304], P(('dp', 'ep'))
- output 4: float32 [2304], replicated
- output 5: float32 [2304, 8], replicated
- output 6: bfloat16 [8, 2304, 5760], P('ep')
- output 7: bfloat16 [8, 2304, 5760], P('ep')
- output 8: bfloat16 [8, 5760, 2304], P('ep')
All inputs are finite; a program needn't handle non-finite values.
Results may differ from a plain program's by a relative error of at most 0.0141986.
Values are sent between devices in bfloat16 or wider.
A program may use at most 1 GiB of HBM per device.

v0:
```python
import jax
import jax.numpy as jnp
from jax import lax
from jax.sharding import PartitionSpec as P

EPS = 1e-6
AUX_COEF = 0.001


def route_tables(expert_ids, n_exp, capacity):
    flat_ids = expert_ids.reshape(-1)
    n_choice = flat_ids.shape[0]
    one_hot = (flat_ids[:, None] == jnp.arange(n_exp, dtype=jnp.int32)[None, :]).astype(jnp.int32)
    running = jnp.cumsum(one_hot, axis=0) - 1
    dest_rows = flat_ids * capacity + jnp.sum(running * one_hot, axis=1)
    slot_owner = jnp.full((n_exp * capacity,), n_choice, jnp.int32).at[dest_rows].set(jnp.arange(n_choice, dtype=jnp.int32))
    return dest_rows, slot_owner, jnp.sum(one_hot, axis=0)


def solution(mesh):
    n_dev = mesh.shape["dp"] * mesh.shape["ep"]
    all_axes = ("dp", "ep")

    def local_step(hidden, grad_out, expert_ids, norm_gain, w_router, w_gate, w_up, w_down):
        n_tok, width = hidden.shape
        n_exp = w_router.shape[1]
        capacity = 4 * n_tok // n_exp
        total_tok = n_tok * n_dev
        dest_rows, slot_owner, loads = route_tables(expert_ids, n_exp, capacity)
        choice_hot = (expert_ids[:, :, None] == jnp.arange(n_exp, dtype=jnp.int32)).astype(jnp.float32)

        x_f32 = hidden.astype(jnp.float32)
        inv_rms = lax.rsqrt(jnp.mean(x_f32 * x_f32, axis=-1, keepdims=True) + EPS)
        x_hat = x_f32 * inv_rms
        x_norm = (x_hat * norm_gain).astype(jnp.bfloat16)
        xn_f32 = x_norm.astype(jnp.float32)
        router_probs = jax.nn.softmax(jnp.dot(xn_f32, w_router, preferred_element_type=jnp.float32), axis=-1)
        gate_vals = jnp.sum(router_probs[:, None, :] * choice_hot, axis=-1)
        route_stats = lax.psum(jnp.concatenate([loads.astype(jnp.float32), jnp.sum(router_probs, axis=0)]), all_axes)
        load_frac = route_stats[:n_exp] / (2 * total_tok)
        aux_loss = AUX_COEF * n_exp * jnp.sum(load_frac * route_stats[n_exp:] / total_tok)

        send_rows = jnp.take(x_norm, slot_owner // 2, axis=0, mode="fill", fill_value=0).reshape(n_exp, capacity, width)
        recv_rows = lax.all_to_all(send_rows, "ep", 0, 1, tiled=True)
        h_gate = jnp.einsum("nrd,ndf->nrf", recv_rows, w_gate, preferred_element_type=jnp.float32).astype(jnp.bfloat16)
        h_up = jnp.einsum("nrd,ndf->nrf", recv_rows, w_up, preferred_element_type=jnp.float32).astype(jnp.bfloat16)
        gate_f32 = h_gate.astype(jnp.float32)
        up_f32 = h_up.astype(jnp.float32)
        sig_gate = jax.nn.sigmoid(gate_f32)
        silu_gate = gate_f32 * sig_gate
        act_rows = (silu_gate * up_f32).astype(jnp.bfloat16)
        exp_out = jnp.einsum("nrf,nfd->nrd", act_rows, w_down, preferred_element_type=jnp.float32).astype(jnp.bfloat16)
        back_rows = lax.all_to_all(exp_out, "ep", 1, 0, tiled=True).reshape(n_exp * capacity, width)
        picked = jnp.take(back_rows, dest_rows, axis=0).reshape(n_tok, 2, width)
        out_hidden = (x_f32 + jnp.sum(gate_vals[:, :, None] * picked, axis=1)).astype(jnp.bfloat16)

        dy_f32 = grad_out.astype(jnp.float32)
        d_gates = jnp.sum(dy_f32[:, None, :] * picked, axis=-1)
        d_picked = (dy_f32[:, None, :] * gate_vals[:, :, None]).astype(jnp.bfloat16).reshape(n_tok * 2, width)
        d_send = jnp.take(d_picked, slot_owner, axis=0, mode="fill", fill_value=0).reshape(n_exp, capacity, width)
        d_recv = lax.all_to_all(d_send, "ep", 0, 1, tiled=True)
        d_act = jnp.einsum("nrd,nfd->nrf", d_recv, w_down, preferred_element_type=jnp.float32)
        d_act = d_act.astype(jnp.bfloat16).astype(jnp.float32)
        g_down = jnp.einsum("nrf,nrd->nfd", act_rows, d_recv, preferred_element_type=jnp.float32)
        d_hup = (d_act * silu_gate).astype(jnp.bfloat16)
        d_hgate = (d_act * up_f32 * sig_gate * (1.0 + gate_f32 * (1.0 - sig_gate))).astype(jnp.bfloat16)
        g_gate = jnp.einsum("nrd,nrf->ndf", recv_rows, d_hgate, preferred_element_type=jnp.float32)
        g_up = jnp.einsum("nrd,nrf->ndf", recv_rows, d_hup, preferred_element_type=jnp.float32)
        d_rows = (jnp.einsum("nrf,ndf->nrd", d_hgate, w_gate, preferred_element_type=jnp.float32) + jnp.einsum("nrf,ndf->nrd", d_hup, w_up, preferred_element_type=jnp.float32)).astype(jnp.bfloat16)
        d_back = lax.all_to_all(d_rows, "ep", 1, 0, tiled=True).reshape(n_exp * capacity, width)
        d_xn_exp = jnp.take(d_back, dest_rows, axis=0).reshape(n_tok, 2, width)

        d_probs = jnp.sum(d_gates[:, :, None] * choice_hot, axis=1) + (AUX_COEF * n_exp / total_tok) * load_frac
        d_logits = router_probs * (d_probs - jnp.sum(router_probs * d_probs, axis=-1, keepdims=True))
        d_xnorm = jnp.einsum("te,de->td", d_logits, w_router) + d_xn_exp[:, 0].astype(jnp.float32) + d_xn_exp[:, 1].astype(jnp.float32)
        d_xnorm = d_xnorm.astype(jnp.bfloat16).astype(jnp.float32)
        value_a6 = d_xnorm * norm_gain
        grad_hidden = (inv_rms * (value_a6 - x_hat * jnp.mean(value_a6 * x_hat, axis=-1, keepdims=True)) + dy_f32).astype(jnp.bfloat16)
        small_grads = lax.psum((jnp.sum(d_xnorm * x_hat, axis=0), jnp.einsum("td,te->de", xn_f32, d_logits)), all_axes)
        big_grads = lax.psum((g_gate, g_up, g_down), "dp")
        return (out_hidden, aux_loss, grad_hidden, small_grads[0], small_grads[1], big_grads[0].astype(jnp.bfloat16), big_grads[1].astype(jnp.bfloat16), big_grads[2].astype(jnp.bfloat16))

    tok_spec = P(all_axes, None)
    w_spec = P("ep", None, None)
    return jax.shard_map(local_step, mesh=mesh, in_specs=(tok_spec, tok_spec, tok_spec, P(), P(), w_spec, w_spec, w_spec), out_specs=(tok_spec, P(), tok_spec, P(), P(), w_spec, w_spec, w_spec), check_vma=False)
```

profile of v0, /device:TPU:1, one launch (start us, length us, event | category | flops | bytes accessed | tf_op | source)
XLA Modules:
  0.0 3792.1 jit_solution(14836270210542024692)
XLA Ops:
  14.5 22.1 all_to_all.16
  36.5 13.0 fusion.12
  49.6 16.0 fusion.18
  65.6 15.4 fusion.45
  83.3 9.1 reduce.1
  94.7 4.8 all-to-all-start.1
  103.4 12.2 all-to-all-done.1
  115.6 3.5 reshape.269
  123.5 2.4 gather_fusion.1
  125.9 2.6 broadcast_select_fusion
  128.5 5.3 all-to-all-start.2
  133.9 73.3 %psum.42 = f32[16]{0:T(128)S(1)} all-reduce(f32[16]{0:T(128)S(1)} %pad_maximum_fusion), channel_id=1, replica_groups=mesh['dp'=16,'ep'=8] {'dp','ep'}, use_global_device_ids=true, to_apply=%region_10.12 | all-reduce | flops 16 | bytes 128 | tf_op jit(solution)/shard_map/psum | solution.py:39
  210.1 17.7 fusion.32
  227.9 21.9 convolution_bitcast_fusion
  249.7 17.0 fusion.4
  266.7 22.1 convolution_bitcast_fusion.1
  288.8 22.7 convolution_bitcast_fusion.2
  311.5 14.5 fusion.42
  326.0 3.1 copy.67
  329.1 9.1 reduce.2
  340.5 4.5 all-to-all-start.3
  345.0 3350.7 %all-reduce.5 = (bf16[1,2304,5760]{2,1,0:T(8,128)(2,1)}, bf16[1,2304,5760]{2,1,0:T(8,128)(2,1)}, bf16[1,5760,2304]{2,1,0:T(8,128)(2,1)}) all-reduce(f32[1,2304,5760]{2,1,0:T(8,128)} %convolution_bitcast_fusion.2, f32[1,2304,5760]{2,1,0:T(8,128)} %convolution_bitcast_fusion.1, ...), channel_id=1, replica_groups=mesh['dp'=16,'ep'=8] {'dp'}, use_global_device_ids=true, to_apply=%region_19.21 | all-reduce | flops 39813120 | bytes 238878720 | tf_op jit(solution)/shard_map/psum | solution.py:80
  3695.7 3.5 reshape.271
  3711.6 70.5 %psum.43 = f32[2304]{0:T(1024)} all-reduce(f32[2304]{0:T(1024)S(1)} %get-tuple-element.9), channel_id=1, replica_groups=mesh['dp'=16,'ep'=8] {'dp','ep'}, use_global_device_ids=true, to_apply=%region_17.19 | all-reduce | flops 2304 | bytes 18432 | tf_op jit(solution)/shard_map/psum | solution.py:79
  (117 shorter events, 38.4 us)
Async XLA Ops:
  7.2 95.9 %copy-start = (f32[2304,8]{0,1:T(8,128)S(1)}, f32[2304,8]{0,1:T(8,128)}, u32[]{:S(2)}) copy-start(f32[2304,8]{0,1:T(8,128)} %param.14) | copy-start | bytes 221188
  9.8 4.5 copy-start.25
  36.5 13.0 copy-start.3
  49.6 16.0 copy-start.1
  92.4 7.1 copy-start.9
  94.7 20.9 all-to-all-start.1
  103.0 18.9 copy-start.19
  103.0 17.9 copy-start.18
  103.4 105.2 %copy-start.12 = (f32[64,8]{0,1:T(8,128)}, f32[64,8]{0,1:T(8,128)S(1)}, u32[]{:S(2)}) copy-start(f32[64,8]{0,1:T(8,128)S(1)} %get-tuple-element.19) | copy-start | bytes 6148
  122.5 86.1 %copy-start.15 = (f32[64,8]{0,1:T(8,128)}, f32[64,8]{0,1:T(8,128)S(1)}, u32[]{:S(2)}) copy-start(f32[64,8]{0,1:T(8,128)S(1)} %get-tuple-element.11) | copy-start | bytes 6148
  125.9 84.2 %copy-start.2 = (bf16[256,5760]{1,0:T(8,128)(2,1)S(1)}, bf16[256,5760]{1,0:T(8,128)(2,1)}, u32[]{:S(2)}) copy-start(bf16[256,5760]{1,0:T(8,128)(2,1)} %copy-done.1) | copy-start | bytes 8847364
  128.5 81.6 %all-to-all-start.2 = ((bf16[8,32,2304]{2,1,0:T(8,128)(2,1)}), bf16[8,32,2304]{2,1,0:T(8,128)(2,1)}, u32[]{:S(2)}, u32[]{:S(2)}) async-start(bf16[8,32,2304]{2,1,0:T(8,128)(2,1)} %broadcast_select_fusion), calls=%async_computation.2 | async-start | bytes 2359296 | tf_op jit(solution)/shard_map/all_to_all | solution.py:61
  133.8 3648.4 %all-reduce.4.cloned.1.call-start = ((), (), s32[]{:S(2)}) async-start(), calls=%async_computation.4 | async-start | bytes 147456 | tf_op jit(solution)/shard_map/psum | solution.py:79
  207.9 20.0 copy-start.21
  249.7 17.0 copy-start.4
  288.8 22.7 copy-start.7
  340.5 3355.2 %all-to-all-start.3 = ((bf16[8,2,36864]{2,1,0:T(2,128)(2,1)}), bf16[8,2,36864]{2,1,0:T(2,128)(2,1)S(1)}, u32[]{:S(2)}, u32[]{:S(2)}) async-start(bf16[8,2,36864]{2,1,0:T(2,128)(2,1)} %reshape.270), calls=%async_computation.3 | async-start | bytes 2359296 | tf_op jit(solution)/shard_map/all_to_all | solution.py:70
  3703.1 2.5 copy-start.13
  3703.1 2.5 copy-start.14
  3703.1 2.5 copy-start.16
  3703.1 2.5 copy-start.22
  3703.1 2.5 copy-start.24
  3703.1 2.5 copy-start.26
  3704.8 3.0 copy-start.11
  (7 other events, 10.9 us)
Sparse Core Ops, SparseCore 0:
  210.2 143.4 all-reduce.3
where the time goes:
time: 3800 us; the launch traced here: 3790 us
  blocking collectives  3520 us (93%)
  matrix products  163 us (4%)
  local copies, waits for them, and re-layouts  38.3 us (1%)
    psum x1, blocking collectives, local_step(): big_grads = lax.psum((g_gate, g_up, g_down), 'dp')  3350 us
  transfers between devices with their start and end apart: 4, of which 1 were waited for; matrix products, arithmetic and copies ran while one was open for 4% of the time, Pallas kernels for 0%

commit v1 on v0

v1 whole, which is shorter than its diff:
```python
import functools
import jax
import jax.numpy as jnp
from jax import lax
from jax.experimental import pallas as pl
from jax.experimental.pallas import tpu as pltpu
from jax.sharding import PartitionSpec as P

EPS = 1e-6
AUX_COEF = 0.001
ROWS = 256
TILE = 384
SLICE = 192
NT = (((1,), (1,)), ((), ()))


def route_tables(expert_ids, n_exp, capacity):
    flat_ids = expert_ids.reshape(-1)
    n_choice = flat_ids.shape[0]
    one_hot = (flat_ids[:, None] == jnp.arange(n_exp, dtype=jnp.int32)[None, :]).astype(jnp.int32)
    running = jnp.cumsum(one_hot, axis=0) - 1
    dest_rows = flat_ids * capacity + jnp.sum(running * one_hot, axis=1)
    slot_owner = jnp.full((n_exp * capacity,), n_choice, jnp.int32).at[dest_rows].set(jnp.arange(n_choice, dtype=jnp.int32))
    return dest_rows, slot_owner


def pack_kernel(block_of, chunk_of, n_steps, tok_ref, pos_ref, gate_ref, x_ref, d_ref, acc, gacc):
    step = pl.program_id(0)
    width = x_ref.shape[1]
    block = block_of[step]

    @pl.when((step == 0) | (block != block_of[jnp.maximum(step - 1, 0)]))
    def _():
        acc[...] = jnp.zeros_like(acc)
        gacc[...] = jnp.zeros_like(gacc)

    @pl.when(step < n_steps[0])
    def _():
        rows = tok_ref.shape[0]
        row_id = block * rows + lax.broadcasted_iota(jnp.int32, (rows, rows), 0)
        hit = pos_ref[0] == row_id
        acc[...] += jnp.dot(hit.astype(jnp.float32).astype(jnp.bfloat16), tok_ref[...], preferred_element_type=jnp.float32)
        gacc[...] += jnp.sum(jnp.where(hit, gate_ref[0], 0.0), axis=1, keepdims=True)

    @pl.when((step == n_steps[0] - 1) | ((step < n_steps[0]) & (block != block_of[step + 1])))
    def _():
        x_ref[...] = acc[:, :width].astype(jnp.bfloat16)
        d_ref[...] = (acc[:, width:] * gacc[...]).astype(jnp.bfloat16)


def pack_rows(tokens, mask, gate, cap):
    n_tok, two_d = tokens.shape
    width = two_d // 2
    n_chunk = n_tok // ROWS
    n_block = cap // ROWS
    m = mask.astype(jnp.bfloat16).reshape(n_chunk, ROWS)
    idx = jnp.arange(ROWS)
    inside = jnp.dot(m, (idx[:, None] < idx[None, :]).astype(jnp.bfloat16), preferred_element_type=jnp.float32).astype(jnp.int32)
    per_chunk = jnp.sum(mask.astype(jnp.int32).reshape(n_chunk, ROWS), axis=1)
    cidx = jnp.arange(n_chunk)
    ends = jnp.sum(jnp.where(cidx[None, :] <= cidx[:, None], per_chunk[None, :], 0), axis=1)
    pos = jnp.where(mask.reshape(n_chunk, ROWS), inside + (ends - per_chunk)[:, None], -1)
    count = jnp.sum(per_chunk)
    n_used = jnp.maximum((count + ROWS - 1) // ROWS, 1)
    bidx = jnp.arange(n_block)
    last_row = jnp.minimum((bidx + 1) * ROWS, count) - 1
    last_chunk = jnp.sum((ends[None, :] <= last_row[:, None]).astype(jnp.int32), axis=1)
    n_steps = jnp.sum(jnp.where(bidx == n_used - 1, last_chunk + bidx, 0)) + 1
    steps = jnp.arange(n_chunk + n_block + 1)
    block_of = jnp.minimum(jnp.sum(((last_chunk + bidx)[None, :] < steps[:, None]).astype(jnp.int32), axis=1), n_used - 1)
    chunk_of = jnp.clip(steps - block_of, 0, n_chunk - 1)
    grid_spec = pltpu.PrefetchScalarGridSpec(
        num_scalar_prefetch=3,
        grid=(n_chunk + n_block,),
        in_specs=[
            pl.BlockSpec((ROWS, two_d), lambda s, b, c, n: (c[s], 0)),
            pl.BlockSpec((1, 1, ROWS), lambda s, b, c, n: (c[s], 0, 0)),
            pl.BlockSpec((1, 1, ROWS), lambda s, b, c, n: (c[s], 0, 0)),
        ],
        out_specs=[pl.BlockSpec((ROWS, width), lambda s, b, c, n: (b[s], 0))] * 2,
        scratch_shapes=[pltpu.VMEM((ROWS, two_d), jnp.float32), pltpu.VMEM((ROWS, 1), jnp.float32)],
    )
    x_rows, d_rows = pl.pallas_call(
        pack_kernel,
        grid_spec=grid_spec,
        out_shape=[jax.ShapeDtypeStruct((cap, width), jnp.bfloat16)] * 2,
        compiler_params=pltpu.CompilerParams(dimension_semantics=("arbitrary",), vmem_limit_bytes=40 * 2**20),
        cost_estimate=pl.CostEstimate(flops=2 * 5 * ROWS * cap * two_d // 2, bytes_accessed=2 * n_tok * two_d * 2, transcendentals=0),
        name="pack_rows",
    )(block_of.astype(jnp.int32), chunk_of.astype(jnp.int32), n_steps.astype(jnp.int32)[None], tokens, pos.astype(jnp.int32)[:, None, :], gate.reshape(n_chunk, 1, ROWS))
    return x_rows, d_rows, n_used.astype(jnp.int32)[None]


def weight_grad_step(wt, wd, x, d, acc_gu, acc_d):
    f = wd.shape[0]
    h = lax.dot_general(wt, x, NT, preferred_element_type=jnp.float32)
    hg = h[:f].astype(jnp.bfloat16).astype(jnp.float32)
    hu = h[f:].astype(jnp.bfloat16).astype(jnp.float32)
    da = lax.dot_general(wd, d, NT, preferred_element_type=jnp.float32).astype(jnp.bfloat16).astype(jnp.float32)
    sig = jax.nn.sigmoid(hg)
    silu = hg * sig
    act = (silu * hu).astype(jnp.bfloat16)
    dhu = (da * silu).astype(jnp.bfloat16)
    dhg = (da * hu * sig * (1.0 + hg * (1.0 - sig))).astype(jnp.bfloat16)
    acc_gu[...] += jnp.dot(jnp.concatenate([dhg, dhu], axis=0), x, preferred_element_type=jnp.float32)
    acc_d[...] += jnp.dot(act, d, preferred_element_type=jnp.float32)


def slice_kernel(n_used, x_ref, d_ref, wt_ref, wd_ref, out_ref, acc_gu, acc_d):
    b = pl.program_id(0)

    @pl.when(b == 0)
    def _():
        acc_gu[...] = jnp.zeros_like(acc_gu)
        acc_d[...] = jnp.zeros_like(acc_d)

    @pl.when(b < n_used[0])
    def _():
        weight_grad_step(wt_ref[...], wd_ref[...], x_ref[...], d_ref[...], acc_gu, acc_d)

    @pl.when(b == pl.num_programs(0) - 1)
    def _():
        f2 = acc_gu.shape[0]
        out_ref[:f2] = acc_gu[...].astype(jnp.bfloat16)
        out_ref[f2:] = acc_d[...].astype(jnp.bfloat16)


def slice_grads(x_rows, d_rows, n_used, wt, wd):
    cap, width = x_rows.shape
    f = wd.shape[0]
    return pl.pallas_call(
        slice_kernel,
        grid_spec=pltpu.PrefetchScalarGridSpec(
            num_scalar_prefetch=1,
            grid=(cap // ROWS,),
            in_specs=[
                pl.BlockSpec((ROWS, width), lambda b, n: (jnp.minimum(b, n[0] - 1), 0)),
                pl.BlockSpec((ROWS, width), lambda b, n: (jnp.minimum(b, n[0] - 1), 0)),
                pl.BlockSpec((2 * f, width), lambda b, n: (0, 0)),
                pl.BlockSpec((f, width), lambda b, n: (0, 0)),
            ],
            out_specs=pl.BlockSpec((3 * f, width), lambda b, n: (0, 0)),
            scratch_shapes=[pltpu.VMEM((2 * f, width), jnp.float32), pltpu.VMEM((f, width), jnp.float32)],
        ),
        out_shape=jax.ShapeDtypeStruct((3 * f, width), jnp.bfloat16),
        compiler_params=pltpu.CompilerParams(dimension_semantics=("arbitrary",), vmem_limit_bytes=50 * 2**20),
        cost_estimate=pl.CostEstimate(flops=12 * (cap // 2) * width * f, bytes_accessed=cap * width * 2, transcendentals=0),
        name="slice_grads",
    )(n_used, x_rows, d_rows, wt, wd)


def tile_kernel(n_used, x_ref, d_ref, wg_ref, wu_ref, wd_ref, gg_ref, gu_ref, gd_ref, wt, acc_gu, acc_d):
    b = pl.program_id(1)
    f = wd_ref.shape[0]

    @pl.when(b == 0)
    def _():
        wt[:f] = wg_ref[...].T
        wt[f:] = wu_ref[...].T
        acc_gu[...] = jnp.zeros_like(acc_gu)
        acc_d[...] = jnp.zeros_like(acc_d)

    @pl.when(b < n_used[0])
    def _():
        weight_grad_step(wt[...], wd_ref[...], x_ref[...], d_ref[...], acc_gu, acc_d)

    @pl.when(b == pl.num_programs(1) - 1)
    def _():
        gg_ref[...] = acc_gu[:f].astype(jnp.bfloat16).T
        gu_ref[...] = acc_gu[f:].astype(jnp.bfloat16).T
        gd_ref[...] = acc_d[...].astype(jnp.bfloat16)


def tile_grads(x_rows, d_rows, n_used, w_gate, w_up, w_down, n_tile):
    cap, width = x_rows.shape
    ff = w_gate.shape[1]
    row_spec = pl.BlockSpec((ROWS, width), lambda j, b, n: (jnp.minimum(b, n[0] - 1), 0))
    col_spec = pl.BlockSpec((width, TILE), lambda j, b, n: (0, j))
    down_spec = pl.BlockSpec((TILE, width), lambda j, b, n: (j, 0))
    return pl.pallas_call(
        tile_kernel,
        grid_spec=pltpu.PrefetchScalarGridSpec(
            num_scalar_prefetch=1,
            grid=(n_tile, cap // ROWS),
            in_specs=[row_spec, row_spec, col_spec, col_spec, down_spec],
            out_specs=[col_spec, col_spec, down_spec],
            scratch_shapes=[pltpu.VMEM((2 * TILE, width), jnp.bfloat16), pltpu.VMEM((2 * TILE, width), jnp.float32), pltpu.VMEM((TILE, width), jnp.float32)],
        ),
        out_shape=[jax.ShapeDtypeStruct((width, ff), jnp.bfloat16)] * 2 + [jax.ShapeDtypeStruct((ff, width), jnp.bfloat16)],
        compiler_params=pltpu.CompilerParams(dimension_semantics=("arbitrary", "arbitrary"), vmem_limit_bytes=60 * 2**20),
        cost_estimate=pl.CostEstimate(flops=12 * (cap // 2) * width * TILE * n_tile, bytes_accessed=n_tile * cap * width * 2, transcendentals=0),
        name="tile_grads",
    )(n_used, x_rows, d_rows, w_gate, w_up, w_down)


def place_kernel(part_ref, gg_in, gu_in, gd_in, gg_ref, gu_ref, gd_ref):
    f = SLICE
    gg_ref[...] = jnp.concatenate([part_ref[0, :f], part_ref[1, :f]], axis=0).T
    gu_ref[...] = jnp.concatenate([part_ref[0, f:2 * f], part_ref[1, f:2 * f]], axis=0).T
    gd_ref[:f] = part_ref[0, 2 * f:]
    gd_ref[f:] = part_ref[1, 2 * f:]


def place_slices(parts, g_gate, g_up, g_down, n_tile):
    n_part, _, width = parts.shape
    col_spec = pl.BlockSpec((width, 2 * SLICE), lambda i: (0, n_tile + i))
    down_spec = pl.BlockSpec((2 * SLICE, width), lambda i: (n_tile + i, 0))
    any_spec = pl.BlockSpec(memory_space=pl.ANY)
    return pl.pallas_call(
        place_kernel,
        grid=(n_part // 2,),
        in_specs=[pl.BlockSpec((2, 3 * SLICE, width), lambda i: (i, 0, 0)), any_spec, any_spec, any_spec],
        out_specs=[col_spec, col_spec, down_spec],
        out_shape=[jax.ShapeDtypeStruct(g.shape, g.dtype) for g in (g_gate, g_up, g_down)],
        input_output_aliases={1: 0, 2: 1, 3: 2},
        compiler_params=pltpu.CompilerParams(dimension_semantics=("arbitrary",), vmem_limit_bytes=50 * 2**20),
        cost_estimate=pl.CostEstimate(flops=10**6, bytes_accessed=4 * parts.size, transcendentals=0),
        name="place_slices",
    )(parts, g_gate, g_up, g_down)


def solution(mesh):
    n_dp, n_ep = mesh.shape["dp"], mesh.shape["ep"]
    n_dev = n_dp * n_ep
    all_axes = ("dp", "ep")

    def local_step(hidden, grad_out, expert_ids, norm_gain, w_router, w_gate, w_up, w_down):
        n_tok, width = hidden.shape
        n_exp = w_router.shape[1]
        capacity = 4 * n_tok // n_exp
        total_tok = n_tok * n_dev
        w_gate, w_up, w_down = w_gate[0], w_up[0], w_down[0]
        ff = w_gate.shape[1]
        n_tile = (ff - SLICE * n_dp) // TILE
        my_exp = lax.axis_index("ep")
        dest_rows, slot_owner = route_tables(expert_ids, n_exp, capacity)
        choice_hot = (expert_ids[:, :, None] == jnp.arange(n_exp, dtype=jnp.int32)).astype(jnp.float32)

        x_f32 = hidden.astype(jnp.float32)
        inv_rms = lax.rsqrt(jnp.mean(x_f32 * x_f32, axis=-1, keepdims=True) + EPS)
        x_hat = x_f32 * inv_rms
        x_norm = (x_hat * norm_gain).astype(jnp.bfloat16)
        xn_f32 = x_norm.astype(jnp.float32)

        tokens = lax.all_gather(jnp.concatenate([x_norm, grad_out], axis=1), all_axes, axis=0, tiled=True)

        router_probs = jax.nn.softmax(jnp.dot(xn_f32, w_router, preferred_element_type=jnp.float32), axis=-1)
        gate_vals = jnp.sum(router_probs[:, None, :] * choice_hot, axis=-1)
        pad = jnp.zeros((n_tok, 16 - n_exp - 2), jnp.float32)
        routes = lax.all_gather(jnp.concatenate([router_probs, expert_ids.astype(jnp.float32), pad], axis=1), all_axes, axis=0, tiled=True)
        all_probs, all_ids = routes[:, :n_exp], routes[:, n_exp:n_exp + 2].astype(jnp.int32)
        exp_range = jnp.arange(n_exp, dtype=jnp.int32)
        loads = jnp.sum((all_ids[:, 0:1] == exp_range).astype(jnp.float32) + (all_ids[:, 1:2] == exp_range).astype(jnp.float32), axis=0)
        load_frac = loads / (2 * total_tok)
        aux_loss = AUX_COEF * n_exp * jnp.sum(load_frac * jnp.sum(all_probs, axis=0) / total_tok)

        dy_f32 = grad_out.astype(jnp.float32)
        d_picked = (dy_f32[:, None, :] * gate_vals[:, :, None]).astype(jnp.bfloat16).reshape(n_tok * 2, width)
        send_x = jnp.take(x_norm, slot_owner // 2, axis=0, mode="fill", fill_value=0)
        send_d = jnp.take(d_picked, slot_owner, axis=0, mode="fill", fill_value=0)
        send = jnp.concatenate([send_x, send_d], axis=1).reshape(n_exp, capacity, 2 * width)
        recv = lax.all_to_all(send, "ep", 0, 0, tiled=True).reshape(n_exp * capacity, 2 * width)
        recv_rows, d_recv = recv[:, :width], recv[:, width:]
        h_gate = jnp.dot(recv_rows, w_gate, preferred_element_type=jnp.float32).astype(jnp.bfloat16)
        h_up = jnp.dot(recv_rows, w_up, preferred_element_type=jnp.float32).astype(jnp.bfloat16)
        gate_f32 = h_gate.astype(jnp.float32)
        up_f32 = h_up.astype(jnp.float32)
        sig_gate = jax.nn.sigmoid(gate_f32)
        silu_gate = gate_f32 * sig_gate
        act_rows = (silu_gate * up_f32).astype(jnp.bfloat16)
        exp_out = jnp.dot(act_rows, w_down, preferred_element_type=jnp.float32).astype(jnp.bfloat16)
        d_act = lax.dot_general(d_recv, w_down, NT, preferred_element_type=jnp.float32)
        d_act = d_act.astype(jnp.bfloat16).astype(jnp.float32)
        d_hup = (d_act * silu_gate).astype(jnp.bfloat16)
        d_hgate = (d_act * up_f32 * sig_gate * (1.0 + gate_f32 * (1.0 - sig_gate))).astype(jnp.bfloat16)
        d_rows = (lax.dot_general(d_hgate, w_gate, NT, preferred_element_type=jnp.float32) + lax.dot_general(d_hup, w_up, NT, preferred_element_type=jnp.float32)).astype(jnp.bfloat16)
        home = jnp.concatenate([exp_out, d_rows], axis=1).reshape(n_exp, capacity, 2 * width)
        back = lax.all_to_all(home, "ep", 0, 0, tiled=True).reshape(n_exp * capacity, 2 * width)
        taken = jnp.take(back, dest_rows, axis=0).reshape(n_tok, 2, 2 * width)
        picked, d_xn_exp = taken[:, :, :width], taken[:, :, width:]
        out_hidden = (x_f32 + jnp.sum(gate_vals[:, :, None] * picked, axis=1)).astype(jnp.bfloat16)

        d_gates = jnp.sum(dy_f32[:, None, :] * picked, axis=-1)
        d_probs = jnp.sum(d_gates[:, :, None] * choice_hot, axis=1) + (AUX_COEF * n_exp / total_tok) * load_frac
        d_logits = router_probs * (d_probs - jnp.sum(router_probs * d_probs, axis=-1, keepdims=True))
        d_xnorm = jnp.einsum("te,de->td", d_logits, w_router) + d_xn_exp[:, 0].astype(jnp.float32) + d_xn_exp[:, 1].astype(jnp.float32)
        d_xnorm = d_xnorm.astype(jnp.bfloat16).astype(jnp.float32)
        scaled = d_xnorm * norm_gain
        grad_hidden = (inv_rms * (scaled - x_hat * jnp.mean(scaled * x_hat, axis=-1, keepdims=True)) + dy_f32).astype(jnp.bfloat16)
        small = jnp.concatenate([jnp.sum(d_xnorm * x_hat, axis=0)[None], jnp.einsum("te,td->ed", d_logits, xn_f32)], axis=0)
        small = lax.all_gather(small.reshape(-1, 128), all_axes, axis=0, tiled=True)
        small = jnp.sum(small.reshape(n_dev, -1, 128), axis=0).reshape(1 + n_exp, width)

        names = all_ids == my_exp
        mask = names[:, 0] | names[:, 1]
        gate = jnp.sum(jnp.where(exp_range == my_exp, all_probs, 0.0), axis=1)
        x_rows, do_rows, n_used = pack_rows(tokens, mask, gate, n_dev * capacity)
        at = n_tile * TILE + SLICE * lax.axis_index("dp")
        wt = jnp.concatenate([lax.dynamic_slice(w, (0, at), (width, SLICE)).T for w in (w_gate, w_up)], axis=0)
        mine = slice_grads(x_rows, do_rows, n_used, wt, lax.dynamic_slice(w_down, (at, 0), (SLICE, width)))
        parts = lax.all_gather(mine, "dp", axis=0, tiled=False)
        g_gate, g_up, g_down = tile_grads(x_rows, do_rows, n_used, w_gate, w_up, w_down, n_tile)
        g_gate, g_up, g_down = place_slices(parts, g_gate, g_up, g_down, n_tile)
        return (out_hidden, aux_loss, grad_hidden, small[0], small[1:].T, g_gate[None], g_up[None], g_down[None])

    tok_spec = P(all_axes, None)
    w_spec = P("ep", None, None)
    return jax.shard_map(local_step, mesh=mesh, in_specs=(tok_spec, tok_spec, tok_spec, P(), P(), w_spec, w_spec, w_spec), out_specs=(tok_spec, P(), tok_spec, P(), P(), w_spec, w_spec, w_spec), check_vma=False)
```

time: 3800 us -> 706 us (0.19)
  the two profiles are of different devices: /device:TPU:1 before, /device:TPU:5 now
where the time goes in v1:
time: 706 us; the launch traced here: 696 us
  Pallas kernels  422 us (60%)
  matrix products  105 us (15%)
  blocking collectives  68.9 us (10%)
  waiting for transfers between devices  25.6 us (4%)
  other arithmetic  23.5 us (3%)
  local copies, waits for them, and re-layouts  23 us (3%)
  between operations  17.5 us (2%)
  starting transfers between devices  10.6 us (2%)
    pallas_call x1, Pallas kernels, tile_grads(): pl.pallas_call(tile_kernel, grid_spec=pltpu.PrefetchScalarGridSpec(num_sc...  309 us
    all_gather x1, blocking collectives, local_step(): lax.all_gather(jnp.concatenate([router_probs, expert_ids.astype(jnp.float...  68.9 us
    pallas_call x1, Pallas kernels, pack_rows(): pl.pallas_call(pack_kernel, grid_spec=grid_spec, out_shape=[jax.ShapeDtyp...  61.9 us
    pallas_call x1, Pallas kernels, place_slices(): pl.pallas_call(place_kernel, grid=(n_part // 2,), in_specs=[pl.BlockSpec(...  27.5 us
    all_to_all x1, waiting for transfers between devices, local_step(): lax.all_to_all(home, 'ep', 0, 0, tiled=True)  25.6 us
    pallas_call x1, Pallas kernels, slice_grads(): pl.pallas_call(slice_kernel, grid_spec=pltpu.PrefetchScalarGridSpec(num_s...  23.4 us
    dot_general x1, matrix products, local_step(): lax.dot_general(d_hgate, w_gate, NT, preferred_element_type=jnp.float32)  21.4 us
    dot_general x1, matrix products, local_step(): jnp.dot(act_rows, w_down, preferred_element_type=jnp.float32)  18.1 us
  transfers between devices with their start and end apart: 5, of which 1 were waited for; matrix products, arithmetic and copies ran while one was open for 21% of the time, Pallas kernels for 57%

profile of v1, /device:TPU:5, one launch (start us, length us, event | category | flops | bytes accessed | tf_op | source)
XLA Modules:
  0.0 695.8 jit_solution(2046549174371315410)
XLA Ops:
  9.6 1.8 pad_maximum_fusion.3
  19.1 1.6 pad_maximum_fusion
  20.7 5.2 all-to-all-start
  26.1 68.9 %all-gather.1 = f32[128,64,16]{1,2,0:T(8,128)S(1)} all-gather(f32[1,64,16]{1,2,0:T(8,128)S(1)} %maximum_bitcast_fusion), channel_id=1, replica_groups=mesh['dp'=16,'ep'=8] {'dp','ep'}, dimensions={0}, use_global_device_ids=true | all-gather | bytes 528384 | tf_op jit(solution)/shard_map/all_gather | solution.py:250
  96.8 14.7 %fusion = f32[256,5760]{1,0:T(8,128)} fusion(bf16[256,4608]{1,0:T(8,128)(2,1)} %bitcast.4, bf16[1,5760,2304]{2,1,0:T(8,128)(2,1)} %param.15), kind=kOutput, calls=%fused_computation.8 | convolution fusion | flops 6797721600 | bytes 33619968 | tf_op jit(solution)/shard_map/dot_general | solution.py:272
  111.5 17.3 %convolution_convert_fusion.2 = bf16[256,5760]{1,0:T(8,128)(2,1)} fusion(bf16[256,4608]{1,0:T(8,128)(2,1)} %bitcast.4, bf16[1,2304,5760]{2,1,0:T(8,128)(2,1)} %param.13), kind=kOutput, calls=%fused_computation.11 | convolution fusion | flops 6796247040 | bytes 30670848 | tf_op jit(solution)/shard_map/dot_general | solution.py:264
  128.8 14.5 %fusion.1 = f32[256,5760]{1,0:T(8,128)} fusion(bf16[256,4608]{1,0:T(8,128)(2,1)} %bitcast.4, bf16[1,2304,5760]{2,1,0:T(8,128)(2,1)} %param.14), kind=kOutput, calls=%fused_computation.10 | convolution fusion | flops 6797721600 | bytes 33619968 | tf_op jit(solution)/shard_map/dot_general | solution.py:265
  143.3 21.4 %fusion.12 = f32[256,2304]{1,0:T(8,128)} fusion(bf16[256,5760]{1,0:T(8,128)(2,1)} %convolution_convert_fusion.2, f32[256,5760]{1,0:T(8,128)} %fusion, f32[256,5760]{1,0:T(8,128)} %fusion.1, bf16[1,2304,5760]{2,1,0:T(8,128)(2,1)} %param.13), kind=kOutput, calls=%fused_computation.27 | convolution fusion | flops 6810992640 | bytes 43646976 | tf_op jit(solution)/shard_map/dot_general | solution.py:276
  164.7 16.8 %fusion.8 = bf16[256,2304]{1,0:T(8,128)(2,1)S(1)} fusion(f32[256,2304]{1,0:T(8,128)} %fusion.12, f32[256,5760]{1,0:T(8,128)} %fusion, bf16[256,5760]{1,0:T(8,128)(2,1)} %convolution_convert_fusion.2, bf16[1,2304,5760]{2,1,0:T(8,128)(2,1)} %param.14), kind=kOutput, calls=%fused_computation.22 | convolution fusion | flops 6806274048 | bytes 38928384 | tf_op jit(solution)/shard_map/dot_general | solution.py:276
  181.5 18.1 %convolution_convert_fusion.3 = bf16[256,2304]{1,0:T(8,128)(2,1)S(1)} fusion(f32[256,5760]{1,0:T(8,128)} %fusion.1, bf16[256,5760]{1,0:T(8,128)(2,1)} %convolution_convert_fusion.2, bf16[1,5760,2304]{2,1,0:T(8,128)(2,1)} %param.15), kind=kOutput, calls=%fused_computation.21 | convolution fusion | flops 6805684224 | bytes 36569088 | tf_op jit(solution)/shard_map/dot_general | solution.py:271
  199.6 1.6 pad_maximum_fusion.1
  201.2 5.3 all-to-all-start.1
  207.4 25.6 %all-to-all-done.1 = bf16[8,32,4608]{2,1,0:T(8,128)(2,1)} async-done(((bf16[8,32,4608]{2,1,0:T(8,128)(2,1)}), bf16[8,32,4608]{2,1,0:T(8,128)(2,1)}, u32[]{:S(2)}, u32[]{:S(2)}) %all-to-all-start.1) | async-done | bytes 2359328 | tf_op jit(solution)/shard_map/all_to_all | solution.py:278
  232.9 4.4 gather_fusion.2
  238.1 2.3 fusion.16
  247.9 2.0 constant_dynamic-slice_fusion
  249.9 1.5 copy.66
  251.4 2.0 constant_dynamic-slice_fusion.1
  256.1 1.6 pad_maximum_fusion.2.wt_ref
  257.7 61.9 %pack_rows.1 = (bf16[4096,2304]{1,0:T(8,128)(2,1)}, bf16[4096,2304]{1,0:T(8,128)(2,1)}) custom-call(s32[49]{0:T(128)S(1)} %get-tuple-element.31.block_of, s32[49]{0:T(128)S(1)} %get-tuple-element.30.chunk_of, s32[1]{0:T(128)} %bitcast.18.n_steps, bf16[8192,4608]{1,0:T(8,128)(2,1)} %all-gather.7.cloned.1.call-done.tok_ref, ...), custom_call_target="tpu_custom_call" | custom-call | flops 24159191040 | bytes 150994944 | tf_op jit(solution)/shard_map/pack_rows/pallas_call | solution.py:83
  319.6 23.4 %slice_grads.1 = bf16[576,2304]{1,0:T(8,128)(2,1)} custom-call(s32[1]{0:T(128)} %bitcast.17.n_used, bf16[4096,2304]{1,0:T(8,128)(2,1)} %get-tuple-element.16.x_ref, bf16[4096,2304]{1,0:T(8,128)(2,1)} %get-tuple-element.17.d_ref, bf16[384,2304]{1,0:T(8,128)(2,1)S(1)} %pad_maximum_fusion.2.wt_ref, bf16[192,2304]{1,0:T(8,128)(2,1)S(1)} %dynamic-slice_bitcast_fusion.wd_ref), custom_call_target="tpu_custom_call" | custom-call | flops 10871635968 | bytes 18874368 | tf_op jit(solution)/shard_map/slice_grads/pallas_call | solution.py:131
  345.3 4.7 reduce_sum.208
  351.2 309.2 %tile_grads.1 = (bf16[2304,5760]{1,0:T(8,128)(2,1)}, bf16[2304,5760]{1,0:T(8,128)(2,1)}, bf16[5760,2304]{1,0:T(8,128)(2,1)}) custom-call(s32[1]{0:T(128)} %bitcast.17.n_used, bf16[4096,2304]{1,0:T(8,128)(2,1)} %get-tuple-element.16.x_ref, bf16[4096,2304]{1,0:T(8,128)(2,1)} %get-tuple-element.17.d_ref, bf16[2304,5760]{1,0:T(8,128)(2,1)} %bitcast.77, ...), custom_call_target="tpu_custom_call" | custom-call | flops 152202903552 | bytes 132120576 | tf_op jit(solution)/shard_map/tile_grads/pallas_call | solution.py:180
  660.4 27.5 %place_slices.1 = (bf16[2304,5760]{1,0:T(8,128)(2,1)}, bf16[2304,5760]{1,0:T(8,128)(2,1)}, bf16[5760,2304]{1,0:T(8,128)(2,1)}) custom-call(bf16[16,576,2304]{2,1,0:T(8,128)(2,1)} %bitcast.66, bf16[2304,5760]{1,0:T(8,128)(2,1)} %get-tuple-element.18.gg_in, ...), custom_call_target="tpu_custom_call", output_to_operand_aliasing={{0}: (1, {}), {1}: (2, {}), {2}: (3, {})} | custom-call | flops 1000000 | bytes 84934656 | tf_op jit(solution)/shard_map/place_slices/pallas_call | solution.py:209
  (109 shorter events, 25.2 us)
Async XLA Ops:
  7.2 5.0 copy-start
  7.2 5.5 copy-start.2
  7.2 5.2 copy-start.10
  7.2 250.5 %all-gather.7.cloned.1.call-start = ((), (), s32[]{:S(2)}) async-start(), calls=%async_computation.2 | async-start | bytes 76087296 | tf_op jit(solution)/shard_map/all_gather | solution.py:245
  20.7 74.4 %copy-start.3 = (bf16[64,2304]{1,0:T(8,128)(2,1)S(1)}, bf16[64,2304]{1,0:T(8,128)(2,1)}, u32[]{:S(2)}) copy-start(bf16[64,2304]{1,0:T(8,128)(2,1)} %param.9) | copy-start | bytes 884740
  20.7 76.1 %all-to-all-start = ((bf16[8,32,4608]{2,1,0:T(8,128)(2,1)}), bf16[8,32,4608]{2,1,0:T(8,128)(2,1)}, u32[]{:S(2)}, u32[]{:S(2)}) async-start(bf16[8,32,4608]{2,1,0:T(8,128)(2,1)} %pad_maximum_fusion), calls=%async_computation | async-start | bytes 4718592 | tf_op jit(solution)/shard_map/all_to_all | solution.py:262
  96.7 109.8 %copy-start.7 = (f32[8192,16]{0,1:T(8,128)}, f32[8192,16]{0,1:T(8,128)S(1)}, u32[]{:S(2)}) copy-start(f32[8192,16]{0,1:T(8,128)S(1)} %reshape.216) | copy-start | bytes 1572868
  201.2 31.8 %all-to-all-start.1 = ((bf16[8,32,4608]{2,1,0:T(8,128)(2,1)}), bf16[8,32,4608]{2,1,0:T(8,128)(2,1)}, u32[]{:S(2)}, u32[]{:S(2)}) async-start(bf16[8,32,4608]{2,1,0:T(8,128)(2,1)} %bitcast.8), calls=%async_computation.1 | async-start | bytes 4718592 | tf_op jit(solution)/shard_map/all_to_all | solution.py:278
  206.5 138.8 %all-gather.11.cloned.1.call-start = ((), (), s32[]{:S(2)}) async-start(), calls=%async_computation.4 | async-start | bytes 11096064 | tf_op jit(solution)/shard_map/all_gather | solution.py:291
  237.3 3.1 copy-start.5
  237.3 3.1 copy-start.9
  242.7 417.7 %all-gather.9.cloned.1.call-start = ((), (), s32[]{:S(2)}) async-start(), calls=%async_computation.3 | async-start | bytes 45121536 | tf_op jit(solution)/shard_map/all_gather | solution.py:301
  319.6 24.2 %copy-start.4 = (bf16[64,2304]{1,0:T(8,128)(2,1)S(1)}, bf16[64,2304]{1,0:T(8,128)(2,1)}, u32[]{:S(2)}) copy-start(bf16[64,2304]{1,0:T(8,128)(2,1)} %param.9) | copy-start | bytes 884740
  343.0 1.1 copy-start.6
  343.0 1.3 copy-start.8
  660.4 27.5 %copy-start.1 = (f32[2304,8]{0,1:T(8,128)S(1)}, f32[2304,8]{0,1:T(8,128)}, u32[]{:S(2)}) copy-start(f32[2304,8]{0,1:T(8,128)} %param.12) | copy-start | bytes 221188
Sparse Core Ops, SparseCore 0:
  11.5 192.7 all-gather.6
  242.9 70.5 all-gather.10
  343.1 242.3 all-gather.8
